TPU v7x, 32 devices: a whole 2x2x4 slice. The times are simulated.
32 devices in a mesh: dom: 32 (over z, y, x, core).
Axes of the slice: x: 2, y: 2, z: 4, core: 2. Of those that a mesh axis runs over, the one named last changes fastest.
Arguments:
- start_point: float32 [16384, 128], P('dom'), may hold values from -6 to 6
- residual: float32 [16384, 128], P('dom'), may hold values from -40 to 40
- direction: float32 [16384, 128], P('dom'), may hold values from -40 to 40
- send_list: int32 [32, 4, 3], P('dom'), may hold values from 0 to 3, as said below
- block_cols: int32 [128, 6], P('dom'), may hold values from 0 to 15, as said below
- block_vals: float32 [128, 6, 128, 128], P('dom'), may hold values from -0.2 to 8.1, as said below
Outputs:
- new_point: float32 [16384, 128], P('dom')
- new_residual: float32 [16384, 128], P('dom')
- new_direction: float32 [16384, 128], P('dom')
Inputs may be any that keep to these rules, and one draw needn't show every extreme that they name: send_list[t, m] lists, in its first entries, the distinct blocks of partition t that the partition at offset -off (off as in the first step) reads; between 1 and 3 of them are read for each pair, and some pair reads 3; the other entries are valid block numbers that are never read. `block_cols`: entry 0 of a block row names the row's own block; a block that couples two partitions appears in both partitions' rows, transposed; the assembled matrix is symmetric positive definite. `block_vals`: stored blocks that no coupling uses are zero.
All inputs are finite; a program needn't handle non-finite values.
Results may differ from a plain program's by a relative error of at most 0.0003.
Values sent between devices are 32-bit elements; how exact they have to be, the bound alone decides.
No kernel may reach another device: no remote copies, remote signals or barrier semaphores. Data moves between devices by JAX's collectives and lax.ppermute only.
A program may use at most 128 MiB of HBM per device.

v0:
```python
import jax
import jax.numpy as jnp
from jax import lax
from jax.sharding import PartitionSpec as P

STEPS = 6
BASIS = 13
center_value = 4.5
half_range = 4.5


def from_behind(shard, axis, by):
    peers = lax.axis_size(axis)
    return lax.ppermute(shard, axis, [(i, (i + by) % peers) for i in range(peers)])


def apply_blocks(blocked, send_rows, block_cols, block_vals):
    block_count, block_rows, width = blocked.shape
    highest = lax.Precision.HIGHEST
    flat_rows = blocked.reshape(block_count, block_rows * width)
    hop_count = send_rows.shape[0] // 2
    own_ids = jnp.arange(block_count, dtype=jnp.int32)
    pieces = [flat_rows]
    for slot_index in range(2 * hop_count):
        offset = slot_index + 1 if slot_index < hop_count else hop_count - 1 - slot_index
        chooser = (send_rows[slot_index][:, None] == own_ids[None, :]).astype(jnp.float32)
        outgoing = jnp.dot(chooser, flat_rows, precision=highest)
        pieces.append(from_behind(outgoing, "dom", -offset))
    ghost_table = jnp.concatenate(pieces, axis=0)
    ghost_ids = jnp.arange(ghost_table.shape[0], dtype=jnp.int32)
    running = jnp.zeros((block_count, block_rows, width), jnp.float32)
    for slot_index in range(block_cols.shape[1]):
        chooser = (block_cols[:, slot_index][:, None] == ghost_ids[None, :]).astype(jnp.float32)
        picked = jnp.dot(chooser, ghost_table, precision=highest).reshape(
            block_count, block_rows, width
        )
        running = running + jnp.einsum(
            "icb,ibw->icw", block_vals[:, slot_index], picked, precision=highest
        )
    return running


def next_vector(vector, send_rows, block_cols, block_vals):
    block_count = block_vals.shape[0]
    block_rows = block_vals.shape[2]
    blocked = vector.reshape(block_count, block_rows, vector.shape[1])
    image_part = apply_blocks(blocked, send_rows, block_cols, block_vals).reshape(vector.shape)
    return (image_part - center_value * vector) / half_range


def basis_change():
    positions = jnp.arange(BASIS)
    row_ids = positions[:, None]
    col_ids = positions[None, :]
    active = (col_ids < STEPS) | (col_ids > STEPS) & (col_ids < BASIS - 1)
    change_table = jnp.where(active & (row_ids == col_ids), center_value, 0.0)
    change_table = change_table + jnp.where(active & (row_ids == col_ids + 1), half_range, 0.0)
    return change_table.astype(jnp.float32)


def coefficient_steps(gram_matrix):
    change_table = basis_change()
    column_count = gram_matrix.shape[0]
    positions = jnp.arange(BASIS)
    point_c = jnp.zeros((column_count, BASIS), jnp.float32)
    resid_c = jnp.broadcast_to((positions == STEPS + 1).astype(jnp.float32), (column_count, BASIS))
    direc_c = jnp.broadcast_to((positions == 0).astype(jnp.float32), (column_count, BASIS))
    highest = lax.Precision.HIGHEST
    for step_index in range(STEPS):
        current = jnp.sum(
            resid_c * jnp.einsum("nab,nb->na", gram_matrix, resid_c, precision=highest), axis=1
        )
        moved_dir = jnp.einsum("ab,nb->na", change_table, direc_c, precision=highest)
        curvature = jnp.sum(
            direc_c * jnp.einsum("nab,nb->na", gram_matrix, moved_dir, precision=highest), axis=1
        )
        alpha_step = current / curvature
        point_c = point_c + alpha_step[:, None] * direc_c
        resid_c = resid_c - alpha_step[:, None] * moved_dir
        following = jnp.sum(
            resid_c * jnp.einsum("nab,nb->na", gram_matrix, resid_c, precision=highest), axis=1
        )
        direc_c = resid_c + (following / current)[:, None] * direc_c
    return (point_c, resid_c, direc_c)


def shards(start_point, residual, direction, send_list, block_cols, block_vals):
    send_rows = send_list[0]
    p_basis = [direction]
    r_basis = [residual]
    for power_step in range(STEPS):
        p_basis.append(next_vector(p_basis[-1], send_rows, block_cols, block_vals))
    for power_step in range(STEPS - 1):
        r_basis.append(next_vector(r_basis[-1], send_rows, block_cols, block_vals))
    basis_stack = jnp.stack(p_basis + r_basis)
    local_gram = jnp.einsum(
        "arn,brn->nab", basis_stack, basis_stack, precision=lax.Precision.HIGHEST
    )
    gram_matrix = lax.psum(local_gram, "dom")
    point_c, resid_c, direc_c = coefficient_steps(gram_matrix)
    highest = lax.Precision.HIGHEST
    new_point = start_point + jnp.einsum("na,arn->rn", point_c, basis_stack, precision=highest)
    new_residual = jnp.einsum("na,arn->rn", resid_c, basis_stack, precision=highest)
    new_direction = jnp.einsum("na,arn->rn", direc_c, basis_stack, precision=highest)
    return (new_point, new_residual, new_direction)


def solution(mesh):
    return jax.shard_map(
        shards,
        mesh=mesh,
        in_specs=(
            P("dom", None),
            P("dom", None),
            P("dom", None),
            P("dom", None, None),
            P("dom", None),
            P("dom", None, None, None),
        ),
        out_specs=(P("dom", None), P("dom", None), P("dom", None)),
        check_vma=False,
    )
```

profile of v0, /device:TPU:0, one launch (start us, length us, event | category | flops | bytes accessed | tf_op | source)
XLA Modules:
  0.0 516.2 jit_solution(13102410080200635533)
XLA Ops:
  7.2 1.2 slice_reduce_fusion.6
  9.9 6.5 %collective-permute-start.24 = (f32[3,16384]{1,0:T(4,128)S(1)}, f32[3,16384]{1,0:T(4,128)S(1)}, u32[]{:S(2)}, u32[]{:S(2)}) collective-permute-start(f32[3,16384]{1,0:T(4,128)S(1)} %fusion.361), channel_id=1, source_target_pairs={{0,31},{1,0},{2,1},{3,2},{4,3},{5,4},{6,5},{7,6},{8,7},{9,8},{10,9... | collective-permute-start | bytes 589832 | tf_op jit(solution)/shard_map/ppermute | solution.py:14
  18.6 1.3 collective-permute-start.27
  21.1 5.0 collective-permute-start
  32.6 7.7 %collective-permute-start.3 = (f32[3,16384]{1,0:T(4,128)}, f32[3,16384]{1,0:T(4,128)}, u32[]{:S(2)}, u32[]{:S(2)}) collective-permute-start(f32[3,16384]{1,0:T(4,128)} %fusion.334), channel_id=1, source_target_pairs={{0,2},{1,3},{2,4},{3,5},{4,6},{5,7},{6,8},{7,9},{8,10},{9,11},{10,... | collective-permute-start | bytes 589832 | tf_op jit(solution)/shard_map/ppermute | solution.py:14
  40.3 2.2 concatenate.39
  53.3 6.4 %concatenate.33 = f32[16,16384]{1,0:T(8,128)S(1)} concatenate(f32[4,16384]{1,0:T(4,128)S(1)} %reshape_reshape.33, f32[3,16384]{1,0:T(4,128)} %collective-permute-done, f32[3,16384]{1,0:T(4,128)} %collective-permute-done.1, f32[3,16384]{1,0:T(4,128)} %collective-permute-done.2, f32[3,16384]{1,0:T(4,128)} %collective-permute-done.3), dimensions={0} | concatenate | bytes 2097152 | tf_op jit(solution)/shard_map/concatenate | solution.py:29
  69.0 2.6 collective-permute-start.28
  71.7 1.9 collective-permute-start.31
  73.6 5.0 collective-permute-start.4
  81.7 1.9 collective-permute-start.5
  83.7 12.6 %collective-permute-start.7 = (f32[3,16384]{1,0:T(4,128)}, f32[3,16384]{1,0:T(4,128)}, u32[]{:S(2)}, u32[]{:S(2)}) collective-permute-start(f32[3,16384]{1,0:T(4,128)} %fusion.333), channel_id=1, source_target_pairs={{0,2},{1,3},{2,4},{3,5},{4,6},{5,7},{6,8},{7,9},{8,10},{9,11},{10,... | collective-permute-start | bytes 589832 | tf_op jit(solution)/shard_map/ppermute | solution.py:14
  96.2 6.5 %concatenate.40 = f32[16,16384]{1,0:T(8,128)S(1)} concatenate(f32[4,16384]{1,0:T(4,128)S(1)} %reshape_reshape.40, f32[3,16384]{1,0:T(4,128)} %copy-done.37, f32[3,16384]{1,0:T(4,128)} %copy-done.40, f32[3,16384]{1,0:T(4,128)} %copy-done.43, f32[3,16384]{1,0:T(4,128)} %collective-permute-done.31), dimensions={0} | concatenate | bytes 2097152 | tf_op jit(solution)/shard_map/concatenate | solution.py:29
  113.2 6.7 %concatenate.34 = f32[16,16384]{1,0:T(8,128)S(1)} concatenate(f32[4,16384]{1,0:T(4,128)S(1)} %reshape_reshape.34, f32[3,16384]{1,0:T(4,128)} %collective-permute-done.4, f32[3,16384]{1,0:T(4,128)} %collective-permute-done.5, f32[3,16384]{1,0:T(4,128)} %collective-permute-done.6, f32[3,16384]{1,0:T(4,128)} %collective-permute-done.7), dimensions={0} | concatenate | bytes 2097152 | tf_op jit(solution)/shard_map/concatenate | solution.py:29
  130.8 1.7 collective-permute-start.34
  132.9 4.6 collective-permute-start.32
  139.3 1.5 collective-permute-done.34
  140.8 10.1 %collective-permute-start.9 = (f32[3,16384]{1,0:T(4,128)}, f32[3,16384]{1,0:T(4,128)}, u32[]{:S(2)}, u32[]{:S(2)}) collective-permute-start(f32[3,16384]{1,0:T(4,128)} %fusion.354), channel_id=1, source_target_pairs={{0,30},{1,31},{2,0},{3,1},{4,2},{5,3},{6,4},{7,5},{8,6},{9,7},{10,... | collective-permute-start | bytes 589832 | tf_op jit(solution)/shard_map/ppermute | solution.py:14
  151.0 5.4 %collective-permute-start.8 = (f32[3,16384]{1,0:T(4,128)}, f32[3,16384]{1,0:T(4,128)}, u32[]{:S(2)}, u32[]{:S(2)}) collective-permute-start(f32[3,16384]{1,0:T(4,128)} %fusion.365), channel_id=1, source_target_pairs={{0,31},{1,0},{2,1},{3,2},{4,3},{5,4},{6,5},{7,6},{8,7},{9,8},{10,9... | collective-permute-start | bytes 589832 | tf_op jit(solution)/shard_map/ppermute | solution.py:14
  156.4 3.3 concatenate.41
  170.9 6.4 %concatenate.35 = f32[16,16384]{1,0:T(8,128)S(1)} concatenate(f32[4,16384]{1,0:T(4,128)S(1)} %reshape_reshape.35, f32[3,16384]{1,0:T(4,128)} %collective-permute-done.8, f32[3,16384]{1,0:T(4,128)} %collective-permute-done.9, f32[3,16384]{1,0:T(4,128)} %collective-permute-done.10, f32[3,16384]{1,0:T(4,128)} %collective-permute-done.11), dimensions={0} | concatenate | bytes 2097152 | tf_op jit(solution)/shard_map/concatenate | solution.py:29
  188.2 3.5 collective-permute-start.38
  191.7 2.6 collective-permute-start.39
  195.3 4.1 collective-permute-start.12
  201.6 4.5 collective-permute-done.37
  206.1 6.6 %collective-permute-start.15 = (f32[3,16384]{1,0:T(4,128)}, f32[3,16384]{1,0:T(4,128)}, u32[]{:S(2)}, u32[]{:S(2)}) collective-permute-start(f32[3,16384]{1,0:T(4,128)} %fusion.331), channel_id=1, source_target_pairs={{0,2},{1,3},{2,4},{3,5},{4,6},{5,7},{6,8},{7,9},{8,10},{9,11},{10,... | collective-permute-start | bytes 589832 | tf_op jit(solution)/shard_map/ppermute | solution.py:14
  212.7 6.5 %concatenate.42 = f32[16,16384]{1,0:T(8,128)S(1)} concatenate(f32[4,16384]{1,0:T(4,128)S(1)} %reshape_reshape.42, f32[3,16384]{1,0:T(4,128)} %copy-done.38, f32[3,16384]{1,0:T(4,128)} %copy-done.41, f32[3,16384]{1,0:T(4,128)} %copy-done.44, f32[3,16384]{1,0:T(4,128)} %collective-permute-done.39), dimensions={0} | concatenate | bytes 2097152 | tf_op jit(solution)/shard_map/concatenate | solution.py:29
  230.3 6.7 %concatenate.36 = f32[16,16384]{1,0:T(8,128)S(1)} concatenate(f32[4,16384]{1,0:T(4,128)S(1)} %reshape_reshape.36, f32[3,16384]{1,0:T(4,128)} %collective-permute-done.12, f32[3,16384]{1,0:T(4,128)} %collective-permute-done.13, f32[3,16384]{1,0:T(4,128)} %collective-permute-done.14, f32[3,16384]{1,0:T(4,128)} %collective-permute-done.15), dimensions={0} | concatenate | bytes 2097152 | tf_op jit(solution)/shard_map/concatenate | solution.py:29
  246.2 2.7 collective-permute-start.40
  249.2 1.7 collective-permute-start.43
  251.9 5.1 collective-permute-start.16
  259.1 1.4 collective-permute-start.17
  261.5 14.8 %collective-permute-start.19 = (f32[3,16384]{1,0:T(4,128)}, f32[3,16384]{1,0:T(4,128)}, u32[]{:S(2)}, u32[]{:S(2)}) collective-permute-start(f32[3,16384]{1,0:T(4,128)} %fusion.330), channel_id=1, source_target_pairs={{0,2},{1,3},{2,4},{3,5},{4,6},{5,7},{6,8},{7,9},{8,10},{9,11},{10,... | collective-permute-start | bytes 589832 | tf_op jit(solution)/shard_map/ppermute | solution.py:14
  276.4 6.2 %concatenate.43 = f32[16,16384]{1,0:T(8,128)S(1)} concatenate(f32[4,16384]{1,0:T(4,128)S(1)} %reshape_reshape.43, f32[3,16384]{1,0:T(4,128)} %copy-done.39, f32[3,16384]{1,0:T(4,128)} %copy-done.42, f32[3,16384]{1,0:T(4,128)} %copy-done.45, f32[3,16384]{1,0:T(4,128)} %collective-permute-done.43), dimensions={0} | concatenate | bytes 2097152 | tf_op jit(solution)/shard_map/concatenate | solution.py:29
  282.6 1.2 convolution_bitcast_fusion.5
  287.4 1.2 convolution_bitcast_fusion.1
  288.5 1.2 convolution_bitcast_fusion
  289.8 6.4 %concatenate.37 = f32[16,16384]{1,0:T(8,128)S(1)} concatenate(f32[4,16384]{1,0:T(4,128)S(1)} %reshape_reshape.37, f32[3,16384]{1,0:T(4,128)} %collective-permute-done.16, f32[3,16384]{1,0:T(4,128)} %collective-permute-done.17, f32[3,16384]{1,0:T(4,128)} %collective-permute-done.18, f32[3,16384]{1,0:T(4,128)} %collective-permute-done.19), dimensions={0} | concatenate | bytes 2097152 | tf_op jit(solution)/shard_map/concatenate | solution.py:29
  308.4 2.7 collective-permute-start.20
  311.3 1.8 collective-permute-start.23
  314.7 3.0 collective-permute-done.20
  317.6 5.8 %collective-permute-done.21 = f32[3,16384]{1,0:T(4,128)S(1)} collective-permute-done((f32[3,16384]{1,0:T(4,128)}, f32[3,16384]{1,0:T(4,128)S(1)}, u32[]{:S(2)}, u32[]{:S(2)}) %collective-permute-start.21) | collective-permute-done | bytes 196640 | tf_op jit(solution)/shard_map/ppermute | solution.py:14
  324.8 6.2 %concatenate.38 = f32[16,16384]{1,0:T(8,128)S(1)} concatenate(f32[4,16384]{1,0:T(4,128)S(1)} %reshape_reshape.38, f32[3,16384]{1,0:T(4,128)} %copy-done.47, f32[3,16384]{1,0:T(4,128)} %copy-done.49, f32[3,16384]{1,0:T(4,128)} %copy-done.50, f32[3,16384]{1,0:T(4,128)} %collective-permute-done.23), dimensions={0} | concatenate | bytes 2097152 | tf_op jit(solution)/shard_map/concatenate | solution.py:29
  338.0 9.0 %stack.55 = f32[13,512,128]{1,0,2:T(8,128)} concatenate(f32[1,512,128]{1,0,2:T(1,128)S(1)} %copy-done.27, f32[1,512,128]{1,0,2:T(1,128)S(1)} %copy-done.30, f32[1,512,128]{1,0,2:T(1,128)S(1)} %copy-done.32, f32[1,512,128]{1,0,2:T(1,128)S(1)} %copy-done.34, f32[1,512,128]{1,0,2:T(1,128)S(1)} %copy-done.35, f32[1,512,128]{1,0,2:T(1,128)S(1)} %copy.74, f32[1,512,128]{1,0,2:T(1,128)S(1)} %copy.75, ...), dimensions={0} | concatenate | bytes 6815744 | tf_op jit(solution)/shard_map/stack | solution.py:95
  347.0 10.0 %fusion.499 = f32[128,13,13]{2,1,0:T(8,128)} fusion(f32[13,512,128]{1,0,2:T(8,128)} %stack.55), kind=kOutput, calls=%fused_computation.689 | convolution fusion | flops 132907008 | bytes 3494400 | tf_op jit(solution)/shard_map/arn,brn->nab/dot_general | solution.py:96
  357.2 134.9 %all-reduce.2.cloned.1.call-done = f32[128,13,13]{2,1,0:T(8,128)} async-done(((f32[128,13,13]{2,1,0:T(8,128)}), f32[128,13,13]{2,1,0:T(8,128)}) %all-reduce.2.cloned.1.call-update) | async-done | bytes 86544 | tf_op jit(solution)/shard_map/psum | solution.py:99
  492.1 1.9 multiply_reduce_fusion.14
  502.3 4.3 multiply_reduce_fusion
  (496 shorter events, 142.8 us)
Async XLA Ops:
  7.2 484.9 %all-reduce.2.cloned.1.call-start = ((), (), s32[]{:S(2)}) async-start(), calls=%async_computation | async-start | bytes 2097152 | tf_op jit(solution)/shard_map/psum | solution.py:99
  9.9 22.1 %collective-permute-start.24 = (f32[3,16384]{1,0:T(4,128)S(1)}, f32[3,16384]{1,0:T(4,128)S(1)}, u32[]{:S(2)}, u32[]{:S(2)}) collective-permute-start(f32[3,16384]{1,0:T(4,128)S(1)} %fusion.361), channel_id=1, source_target_pairs={{0,31},{1,0},{2,1},{3,2},{4,3},{5,4},{6,5},{7,6},{8,7},{9,8},{10,9... | collective-permute-start | bytes 589832 | tf_op jit(solution)/shard_map/ppermute | solution.py:14
  16.8 15.8 %collective-permute-start.25 = (f32[3,16384]{1,0:T(4,128)S(1)}, f32[3,16384]{1,0:T(4,128)S(1)}, u32[]{:S(2)}, u32[]{:S(2)}) collective-permute-start(f32[3,16384]{1,0:T(4,128)S(1)} %fusion.350), channel_id=1, source_target_pairs={{0,30},{1,31},{2,0},{3,1},{4,2},{5,3},{6,4},{7,5},{8,6},{9,7},{10,... | collective-permute-start | bytes 589832 | tf_op jit(solution)/shard_map/ppermute | solution.py:14
  17.9 14.7 %collective-permute-start.26 = (f32[3,16384]{1,0:T(4,128)S(1)}, f32[3,16384]{1,0:T(4,128)S(1)}, u32[]{:S(2)}, u32[]{:S(2)}) collective-permute-start(f32[3,16384]{1,0:T(4,128)S(1)} %fusion.339), channel_id=1, source_target_pairs={{0,1},{1,2},{2,3},{3,4},{4,5},{5,6},{6,7},{7,8},{8,9},{9,10},{10,1... | collective-permute-start | bytes 589832 | tf_op jit(solution)/shard_map/ppermute | solution.py:14
  18.6 21.8 %collective-permute-start.27 = (f32[3,16384]{1,0:T(4,128)S(1)}, f32[3,16384]{1,0:T(4,128)}, u32[]{:S(2)}, u32[]{:S(2)}) collective-permute-start(f32[3,16384]{1,0:T(4,128)S(1)} %fusion.328), channel_id=1, source_target_pairs={{0,2},{1,3},{2,4},{3,5},{4,6},{5,7},{6,8},{7,9},{8,10},{9,11},{10,... | collective-permute-start | bytes 589832 | tf_op jit(solution)/shard_map/ppermute | solution.py:14
  21.1 32.2 %collective-permute-start = (f32[3,16384]{1,0:T(4,128)}, f32[3,16384]{1,0:T(4,128)}, u32[]{:S(2)}, u32[]{:S(2)}) collective-permute-start(f32[3,16384]{1,0:T(4,128)} %fusion.367), channel_id=1, source_target_pairs={{0,31},{1,0},{2,1},{3,2},{4,3},{5,4},{6,5},{7,6},{8,7},{9,8},{10,9... | collective-permute-start | bytes 589832 | tf_op jit(solution)/shard_map/ppermute | solution.py:14
  26.3 22.2 %copy-start.4 = (f32[512,128]{0,1:T(8,128)}, f32[512,128]{0,1:T(8,128)S(1)}, u32[]{:S(2)}) copy-start(f32[512,128]{0,1:T(8,128)S(1)} %copy.60) | copy-start | bytes 786436
  29.8 35.4 %copy-start.2 = (f32[512,128]{0,1:T(8,128)}, f32[512,128]{0,1:T(8,128)S(1)}, u32[]{:S(2)}) copy-start(f32[512,128]{0,1:T(8,128)S(1)} %copy.47) | copy-start | bytes 786436
  32.0 21.3 %collective-permute-start.1 = (f32[3,16384]{1,0:T(4,128)}, f32[3,16384]{1,0:T(4,128)}, u32[]{:S(2)}, u32[]{:S(2)}) collective-permute-start(f32[3,16384]{1,0:T(4,128)} %fusion.356), channel_id=1, source_target_pairs={{0,30},{1,31},{2,0},{3,1},{4,2},{5,3},{6,4},{7,5},{8,6},{9,7},{10,... | collective-permute-start | bytes 589832 | tf_op jit(solution)/shard_map/ppermute | solution.py:14
  32.6 20.7 %collective-permute-start.2 = (f32[3,16384]{1,0:T(4,128)}, f32[3,16384]{1,0:T(4,128)}, u32[]{:S(2)}, u32[]{:S(2)}) collective-permute-start(f32[3,16384]{1,0:T(4,128)} %fusion.345), channel_id=1, source_target_pairs={{0,1},{1,2},{2,3},{3,4},{4,5},{5,6},{6,7},{7,8},{8,9},{9,10},{10,1... | collective-permute-start | bytes 589832 | tf_op jit(solution)/shard_map/ppermute | solution.py:14
  32.6 20.7 %collective-permute-start.3 = (f32[3,16384]{1,0:T(4,128)}, f32[3,16384]{1,0:T(4,128)}, u32[]{:S(2)}, u32[]{:S(2)}) collective-permute-start(f32[3,16384]{1,0:T(4,128)} %fusion.334), channel_id=1, source_target_pairs={{0,2},{1,3},{2,4},{3,5},{4,6},{5,7},{6,8},{7,9},{8,10},{9,11},{10,... | collective-permute-start | bytes 589832 | tf_op jit(solution)/shard_map/ppermute | solution.py:14
  69.0 12.8 %collective-permute-start.28 = (f32[3,16384]{1,0:T(4,128)S(1)}, f32[3,16384]{1,0:T(4,128)S(1)}, u32[]{:S(2)}, u32[]{:S(2)}) collective-permute-start(f32[3,16384]{1,0:T(4,128)S(1)} %copy-done.56), channel_id=1, source_target_pairs={{0,31},{1,0},{2,1},{3,2},{4,3},{5,4},{6,5},{7,6},{8,7},{9,8},{10,9... | collective-permute-start | bytes 589832 | tf_op jit(solution)/shard_map/ppermute | solution.py:14
  71.5 12.1 %collective-permute-start.29 = (f32[3,16384]{1,0:T(4,128)S(1)}, f32[3,16384]{1,0:T(4,128)S(1)}, u32[]{:S(2)}, u32[]{:S(2)}) collective-permute-start(f32[3,16384]{1,0:T(4,128)S(1)} %copy-done.55), channel_id=1, source_target_pairs={{0,30},{1,31},{2,0},{3,1},{4,2},{5,3},{6,4},{7,5},{8,6},{9,7},{10,... | collective-permute-start | bytes 589832 | tf_op jit(solution)/shard_map/ppermute | solution.py:14
  71.6 12.1 %collective-permute-start.30 = (f32[3,16384]{1,0:T(4,128)S(1)}, f32[3,16384]{1,0:T(4,128)S(1)}, u32[]{:S(2)}, u32[]{:S(2)}) collective-permute-start(f32[3,16384]{1,0:T(4,128)S(1)} %copy-done.53), channel_id=1, source_target_pairs={{0,1},{1,2},{2,3},{3,4},{4,5},{5,6},{6,7},{7,8},{8,9},{9,10},{10,1... | collective-permute-start | bytes 589832 | tf_op jit(solution)/shard_map/ppermute | solution.py:14
  71.7 24.5 %collective-permute-start.31 = (f32[3,16384]{1,0:T(4,128)S(1)}, f32[3,16384]{1,0:T(4,128)}, u32[]{:S(2)}, u32[]{:S(2)}) collective-permute-start(f32[3,16384]{1,0:T(4,128)S(1)} %copy-done.51), channel_id=1, source_target_pairs={{0,2},{1,3},{2,4},{3,5},{4,6},{5,7},{6,8},{7,9},{8,10},{9,11},{10,... | collective-permute-start | bytes 589832 | tf_op jit(solution)/shard_map/ppermute | solution.py:14
  73.6 39.5 %collective-permute-start.4 = (f32[3,16384]{1,0:T(4,128)}, f32[3,16384]{1,0:T(4,128)}, u32[]{:S(2)}, u32[]{:S(2)}) collective-permute-start(f32[3,16384]{1,0:T(4,128)} %fusion.366), channel_id=1, source_target_pairs={{0,31},{1,0},{2,1},{3,2},{4,3},{5,4},{6,5},{7,6},{8,7},{9,8},{10,9... | collective-permute-start | bytes 589832 | tf_op jit(solution)/shard_map/ppermute | solution.py:14
  81.7 31.4 %collective-permute-start.5 = (f32[3,16384]{1,0:T(4,128)}, f32[3,16384]{1,0:T(4,128)}, u32[]{:S(2)}, u32[]{:S(2)}) collective-permute-start(f32[3,16384]{1,0:T(4,128)} %fusion.355), channel_id=1, source_target_pairs={{0,30},{1,31},{2,0},{3,1},{4,2},{5,3},{6,4},{7,5},{8,6},{9,7},{10,... | collective-permute-start | bytes 589832 | tf_op jit(solution)/shard_map/ppermute | solution.py:14
  83.6 29.5 %collective-permute-start.6 = (f32[3,16384]{1,0:T(4,128)}, f32[3,16384]{1,0:T(4,128)}, u32[]{:S(2)}, u32[]{:S(2)}) collective-permute-start(f32[3,16384]{1,0:T(4,128)} %fusion.344), channel_id=1, source_target_pairs={{0,1},{1,2},{2,3},{3,4},{4,5},{5,6},{6,7},{7,8},{8,9},{9,10},{10,1... | collective-permute-start | bytes 589832 | tf_op jit(solution)/shard_map/ppermute | solution.py:14
  83.7 29.5 %collective-permute-start.7 = (f32[3,16384]{1,0:T(4,128)}, f32[3,16384]{1,0:T(4,128)}, u32[]{:S(2)}, u32[]{:S(2)}) collective-permute-start(f32[3,16384]{1,0:T(4,128)} %fusion.333), channel_id=1, source_target_pairs={{0,2},{1,3},{2,4},{3,5},{4,6},{5,7},{6,8},{7,9},{8,10},{9,11},{10,... | collective-permute-start | bytes 589832 | tf_op jit(solution)/shard_map/ppermute | solution.py:14
  129.8 9.1 %collective-permute-start.33 = (f32[3,16384]{1,0:T(4,128)}, f32[3,16384]{1,0:T(4,128)S(1)}, u32[]{:S(2)}, u32[]{:S(2)}) collective-permute-start(f32[3,16384]{1,0:T(4,128)} %fusion.348), channel_id=1, source_target_pairs={{0,30},{1,31},{2,0},{3,1},{4,2},{5,3},{6,4},{7,5},{8,6},{9,7},{10,... | collective-permute-start | bytes 589832 | tf_op jit(solution)/shard_map/ppermute | solution.py:14
  130.8 10.0 %collective-permute-start.34 = (f32[3,16384]{1,0:T(4,128)S(1)}, f32[3,16384]{1,0:T(4,128)S(1)}, u32[]{:S(2)}, u32[]{:S(2)}) collective-permute-start(f32[3,16384]{1,0:T(4,128)S(1)} %copy-done.54), channel_id=1, source_target_pairs={{0,1},{1,2},{2,3},{3,4},{4,5},{5,6},{6,7},{7,8},{8,9},{9,10},{10,1... | collective-permute-start | bytes 589832 | tf_op jit(solution)/shard_map/ppermute | solution.py:14
  132.5 18.5 %collective-permute-start.35 = (f32[3,16384]{1,0:T(4,128)S(1)}, f32[3,16384]{1,0:T(4,128)S(1)}, u32[]{:S(2)}, u32[]{:S(2)}) collective-permute-start(f32[3,16384]{1,0:T(4,128)S(1)} %copy-done.52), channel_id=1, source_target_pairs={{0,2},{1,3},{2,4},{3,5},{4,6},{5,7},{6,8},{7,9},{8,10},{9,11},{10,... | collective-permute-start | bytes 589832 | tf_op jit(solution)/shard_map/ppermute | solution.py:14
  132.9 23.6 %collective-permute-start.32 = (f32[3,16384]{1,0:T(4,128)S(1)}, f32[3,16384]{1,0:T(4,128)}, u32[]{:S(2)}, u32[]{:S(2)}) collective-permute-start(f32[3,16384]{1,0:T(4,128)S(1)} %fusion.359), channel_id=1, source_target_pairs={{0,31},{1,0},{2,1},{3,2},{4,3},{5,4},{6,5},{7,6},{8,7},{9,8},{10,9... | collective-permute-start | bytes 589832 | tf_op jit(solution)/shard_map/ppermute | solution.py:14
  137.5 33.3 %collective-permute-start.10 = (f32[3,16384]{1,0:T(4,128)}, f32[3,16384]{1,0:T(4,128)}, u32[]{:S(2)}, u32[]{:S(2)}) collective-permute-start(f32[3,16384]{1,0:T(4,128)} %fusion.343), channel_id=1, source_target_pairs={{0,1},{1,2},{2,3},{3,4},{4,5},{5,6},{6,7},{7,8},{8,9},{9,10},{10,1... | collective-permute-start | bytes 589832 | tf_op jit(solution)/shard_map/ppermute | solution.py:14
  138.9 32.0 %collective-permute-start.11 = (f32[3,16384]{1,0:T(4,128)}, f32[3,16384]{1,0:T(4,128)}, u32[]{:S(2)}, u32[]{:S(2)}) collective-permute-start(f32[3,16384]{1,0:T(4,128)} %fusion.332), channel_id=1, source_target_pairs={{0,2},{1,3},{2,4},{3,5},{4,6},{5,7},{6,8},{7,9},{8,10},{9,11},{10,... | collective-permute-start | bytes 589832 | tf_op jit(solution)/shard_map/ppermute | solution.py:14
  140.8 30.0 %collective-permute-start.9 = (f32[3,16384]{1,0:T(4,128)}, f32[3,16384]{1,0:T(4,128)}, u32[]{:S(2)}, u32[]{:S(2)}) collective-permute-start(f32[3,16384]{1,0:T(4,128)} %fusion.354), channel_id=1, source_target_pairs={{0,30},{1,31},{2,0},{3,1},{4,2},{5,3},{6,4},{7,5},{8,6},{9,7},{10,... | collective-permute-start | bytes 589832 | tf_op jit(solution)/shard_map/ppermute | solution.py:14
  151.0 19.9 %collective-permute-start.8 = (f32[3,16384]{1,0:T(4,128)}, f32[3,16384]{1,0:T(4,128)}, u32[]{:S(2)}, u32[]{:S(2)}) collective-permute-start(f32[3,16384]{1,0:T(4,128)} %fusion.365), channel_id=1, source_target_pairs={{0,31},{1,0},{2,1},{3,2},{4,3},{5,4},{6,5},{7,6},{8,7},{9,8},{10,9... | collective-permute-start | bytes 589832 | tf_op jit(solution)/shard_map/ppermute | solution.py:14
  187.2 14.3 %collective-permute-start.36 = (f32[3,16384]{1,0:T(4,128)}, f32[3,16384]{1,0:T(4,128)S(1)}, u32[]{:S(2)}, u32[]{:S(2)}) collective-permute-start(f32[3,16384]{1,0:T(4,128)} %fusion.358), channel_id=1, source_target_pairs={{0,31},{1,0},{2,1},{3,2},{4,3},{5,4},{6,5},{7,6},{8,7},{9,8},{10,9... | collective-permute-start | bytes 589832 | tf_op jit(solution)/shard_map/ppermute | solution.py:14
  187.9 18.1 %collective-permute-start.37 = (f32[3,16384]{1,0:T(4,128)}, f32[3,16384]{1,0:T(4,128)S(1)}, u32[]{:S(2)}, u32[]{:S(2)}) collective-permute-start(f32[3,16384]{1,0:T(4,128)} %fusion.347), channel_id=1, source_target_pairs={{0,30},{1,31},{2,0},{3,1},{4,2},{5,3},{6,4},{7,5},{8,6},{9,7},{10,... | collective-permute-start | bytes 589832 | tf_op jit(solution)/shard_map/ppermute | solution.py:14
  188.2 17.9 %collective-permute-start.38 = (f32[3,16384]{1,0:T(4,128)}, f32[3,16384]{1,0:T(4,128)S(1)}, u32[]{:S(2)}, u32[]{:S(2)}) collective-permute-start(f32[3,16384]{1,0:T(4,128)} %fusion.336), channel_id=1, source_target_pairs={{0,1},{1,2},{2,3},{3,4},{4,5},{5,6},{6,7},{7,8},{8,9},{9,10},{10,1... | collective-permute-start | bytes 589832 | tf_op jit(solution)/shard_map/ppermute | solution.py:14
  191.7 20.9 %collective-permute-start.39 = (f32[3,16384]{1,0:T(4,128)}, f32[3,16384]{1,0:T(4,128)}, u32[]{:S(2)}, u32[]{:S(2)}) collective-permute-start(f32[3,16384]{1,0:T(4,128)} %fusion.325), channel_id=1, source_target_pairs={{0,2},{1,3},{2,4},{3,5},{4,6},{5,7},{6,8},{7,9},{8,10},{9,11},{10,... | collective-permute-start | bytes 589832 | tf_op jit(solution)/shard_map/ppermute | solution.py:14
  195.3 35.0 %collective-permute-start.12 = (f32[3,16384]{1,0:T(4,128)}, f32[3,16384]{1,0:T(4,128)}, u32[]{:S(2)}, u32[]{:S(2)}) collective-permute-start(f32[3,16384]{1,0:T(4,128)} %fusion.364), channel_id=1, source_target_pairs={{0,31},{1,0},{2,1},{3,2},{4,3},{5,4},{6,5},{7,6},{8,7},{9,8},{10,9... | collective-permute-start | bytes 589832 | tf_op jit(solution)/shard_map/ppermute | solution.py:14
  201.5 28.7 %collective-permute-start.13 = (f32[3,16384]{1,0:T(4,128)}, f32[3,16384]{1,0:T(4,128)}, u32[]{:S(2)}, u32[]{:S(2)}) collective-permute-start(f32[3,16384]{1,0:T(4,128)} %fusion.353), channel_id=1, source_target_pairs={{0,30},{1,31},{2,0},{3,1},{4,2},{5,3},{6,4},{7,5},{8,6},{9,7},{10,... | collective-permute-start | bytes 589832 | tf_op jit(solution)/shard_map/ppermute | solution.py:14
  206.1 24.2 %collective-permute-start.14 = (f32[3,16384]{1,0:T(4,128)}, f32[3,16384]{1,0:T(4,128)}, u32[]{:S(2)}, u32[]{:S(2)}) collective-permute-start(f32[3,16384]{1,0:T(4,128)} %fusion.342), channel_id=1, source_target_pairs={{0,1},{1,2},{2,3},{3,4},{4,5},{5,6},{6,7},{7,8},{8,9},{9,10},{10,1... | collective-permute-start | bytes 589832 | tf_op jit(solution)/shard_map/ppermute | solution.py:14
  206.1 24.2 %collective-permute-start.15 = (f32[3,16384]{1,0:T(4,128)}, f32[3,16384]{1,0:T(4,128)}, u32[]{:S(2)}, u32[]{:S(2)}) collective-permute-start(f32[3,16384]{1,0:T(4,128)} %fusion.331), channel_id=1, source_target_pairs={{0,2},{1,3},{2,4},{3,5},{4,6},{5,7},{6,8},{7,9},{8,10},{9,11},{10,... | collective-permute-start | bytes 589832 | tf_op jit(solution)/shard_map/ppermute | solution.py:14
  246.2 12.9 %collective-permute-start.40 = (f32[3,16384]{1,0:T(4,128)}, f32[3,16384]{1,0:T(4,128)S(1)}, u32[]{:S(2)}, u32[]{:S(2)}) collective-permute-start(f32[3,16384]{1,0:T(4,128)} %fusion.357), channel_id=1, source_target_pairs={{0,31},{1,0},{2,1},{3,2},{4,3},{5,4},{6,5},{7,6},{8,7},{9,8},{10,9... | collective-permute-start | bytes 589832 | tf_op jit(solution)/shard_map/ppermute | solution.py:14
  248.9 12.6 %collective-permute-start.41 = (f32[3,16384]{1,0:T(4,128)}, f32[3,16384]{1,0:T(4,128)S(1)}, u32[]{:S(2)}, u32[]{:S(2)}) collective-permute-start(f32[3,16384]{1,0:T(4,128)} %fusion.346), channel_id=1, source_target_pairs={{0,30},{1,31},{2,0},{3,1},{4,2},{5,3},{6,4},{7,5},{8,6},{9,7},{10,... | collective-permute-start | bytes 589832 | tf_op jit(solution)/shard_map/ppermute | solution.py:14
  248.9 12.6 %collective-permute-start.42 = (f32[3,16384]{1,0:T(4,128)}, f32[3,16384]{1,0:T(4,128)S(1)}, u32[]{:S(2)}, u32[]{:S(2)}) collective-permute-start(f32[3,16384]{1,0:T(4,128)} %fusion.335), channel_id=1, source_target_pairs={{0,1},{1,2},{2,3},{3,4},{4,5},{5,6},{6,7},{7,8},{8,9},{9,10},{10,1... | collective-permute-start | bytes 589832 | tf_op jit(solution)/shard_map/ppermute | solution.py:14
  249.2 27.2 %collective-permute-start.43 = (f32[3,16384]{1,0:T(4,128)}, f32[3,16384]{1,0:T(4,128)}, u32[]{:S(2)}, u32[]{:S(2)}) collective-permute-start(f32[3,16384]{1,0:T(4,128)} %fusion.324), channel_id=1, source_target_pairs={{0,2},{1,3},{2,4},{3,5},{4,6},{5,7},{6,8},{7,9},{8,10},{9,11},{10,... | collective-permute-start | bytes 589832 | tf_op jit(solution)/shard_map/ppermute | solution.py:14
  251.9 37.8 %collective-permute-start.16 = (f32[3,16384]{1,0:T(4,128)}, f32[3,16384]{1,0:T(4,128)}, u32[]{:S(2)}, u32[]{:S(2)}) collective-permute-start(f32[3,16384]{1,0:T(4,128)} %fusion.363), channel_id=1, source_target_pairs={{0,31},{1,0},{2,1},{3,2},{4,3},{5,4},{6,5},{7,6},{8,7},{9,8},{10,9... | collective-permute-start | bytes 589832 | tf_op jit(solution)/shard_map/ppermute | solution.py:14
  259.1 17.3 %copy-start.39 = (f32[3,16384]{1,0:T(4,128)}, f32[3,16384]{1,0:T(4,128)S(1)}, u32[]{:S(2)}) copy-start(f32[3,16384]{1,0:T(4,128)S(1)} %collective-permute-done.40) | copy-start | bytes 589828
  259.1 30.7 %collective-permute-start.17 = (f32[3,16384]{1,0:T(4,128)}, f32[3,16384]{1,0:T(4,128)}, u32[]{:S(2)}, u32[]{:S(2)}) collective-permute-start(f32[3,16384]{1,0:T(4,128)} %fusion.352), channel_id=1, source_target_pairs={{0,30},{1,31},{2,0},{3,1},{4,2},{5,3},{6,4},{7,5},{8,6},{9,7},{10,... | collective-permute-start | bytes 589832 | tf_op jit(solution)/shard_map/ppermute | solution.py:14
  261.5 28.2 %collective-permute-start.18 = (f32[3,16384]{1,0:T(4,128)}, f32[3,16384]{1,0:T(4,128)}, u32[]{:S(2)}, u32[]{:S(2)}) collective-permute-start(f32[3,16384]{1,0:T(4,128)} %fusion.341), channel_id=1, source_target_pairs={{0,1},{1,2},{2,3},{3,4},{4,5},{5,6},{6,7},{7,8},{8,9},{9,10},{10,1... | collective-permute-start | bytes 589832 | tf_op jit(solution)/shard_map/ppermute | solution.py:14
  261.5 28.2 %collective-permute-start.19 = (f32[3,16384]{1,0:T(4,128)}, f32[3,16384]{1,0:T(4,128)}, u32[]{:S(2)}, u32[]{:S(2)}) collective-permute-start(f32[3,16384]{1,0:T(4,128)} %fusion.330), channel_id=1, source_target_pairs={{0,2},{1,3},{2,4},{3,5},{4,6},{5,7},{6,8},{7,9},{8,10},{9,11},{10,... | collective-permute-start | bytes 589832 | tf_op jit(solution)/shard_map/ppermute | solution.py:14
  308.4 9.2 %collective-permute-start.20 = (f32[3,16384]{1,0:T(4,128)}, f32[3,16384]{1,0:T(4,128)S(1)}, u32[]{:S(2)}, u32[]{:S(2)}) collective-permute-start(f32[3,16384]{1,0:T(4,128)} %fusion.362), channel_id=1, source_target_pairs={{0,31},{1,0},{2,1},{3,2},{4,3},{5,4},{6,5},{7,6},{8,7},{9,8},{10,9... | collective-permute-start | bytes 589832 | tf_op jit(solution)/shard_map/ppermute | solution.py:14
  311.1 12.3 %collective-permute-start.21 = (f32[3,16384]{1,0:T(4,128)}, f32[3,16384]{1,0:T(4,128)S(1)}, u32[]{:S(2)}, u32[]{:S(2)}) collective-permute-start(f32[3,16384]{1,0:T(4,128)} %fusion.351), channel_id=1, source_target_pairs={{0,30},{1,31},{2,0},{3,1},{4,2},{5,3},{6,4},{7,5},{8,6},{9,7},{10,... | collective-permute-start | bytes 589832 | tf_op jit(solution)/shard_map/ppermute | solution.py:14
  311.1 12.3 %collective-permute-start.22 = (f32[3,16384]{1,0:T(4,128)S(1)}, f32[3,16384]{1,0:T(4,128)S(1)}, u32[]{:S(2)}, u32[]{:S(2)}) collective-permute-start(f32[3,16384]{1,0:T(4,128)S(1)} %fusion.340), channel_id=1, source_target_pairs={{0,1},{1,2},{2,3},{3,4},{4,5},{5,6},{6,7},{7,8},{8,9},{9,10},{10,1... | collective-permute-start | bytes 589832 | tf_op jit(solution)/shard_map/ppermute | solution.py:14
  311.3 13.5 %collective-permute-start.23 = (f32[3,16384]{1,0:T(4,128)S(1)}, f32[3,16384]{1,0:T(4,128)}, u32[]{:S(2)}, u32[]{:S(2)}) collective-permute-start(f32[3,16384]{1,0:T(4,128)S(1)} %fusion.329), channel_id=1, source_target_pairs={{0,2},{1,3},{2,4},{3,5},{4,6},{5,7},{6,8},{7,9},{8,10},{9,11},{10,... | collective-permute-start | bytes 589832 | tf_op jit(solution)/shard_map/ppermute | solution.py:14
  (55 other events, 281.2 us)
Sparse Core Ops, SparseCore 0:
  357.2 134.8 all-reduce.1
where the time goes:
time: 523 us; the launch traced here: 516 us
  waiting for transfers between devices  151 us (29%)
  starting transfers between devices  119 us (23%)
  matrix products  117 us (22%)
  local copies, waits for them, and re-layouts  95.6 us (18%)
  other arithmetic  17 us (3%)
  between operations  16.7 us (3%)
    psum x1, waiting for transfers between devices, shards(): gram_matrix = lax.psum(local_gram, 'dom')  135 us
    ppermute x44, starting transfers between devices, from_behind(): lax.ppermute(shard, axis, [(i, (i + by) % peers) for i in range(peers)])  118 us
    concatenate x11, local copies, waits for them, and re-layouts, apply_blocks(): ghost_table = jnp.concatenate(pieces, axis=0)  63.5 us
    dot_general x44, matrix products, apply_blocks(): outgoing = jnp.dot(chooser, flat_rows, precision=highest)  44.7 us
    dot_general x66, matrix products, apply_blocks(): jnp.dot(chooser, ghost_table, precision=highest)  36.4 us
    dot_general x66, matrix products, apply_blocks(): jnp.einsum('icb,ibw->icw', block_vals[:, slot_index], picked, precision=h...  25.3 us
    another operation x14, local copies, waits for them, and re-layouts, shards(): basis_stack = jnp.stack(p_basis + r_basis)  18.5 us
    ppermute x44, waiting for transfers between devices, from_behind(): lax.ppermute(shard, axis, [(i, (i + by) % peers) for i in range(peers)])  16 us
  transfers between devices with their start and end apart: 45, of which 7 were waited for; matrix products, arithmetic and copies ran while one was open for 18% of the time, Pallas kernels for 0%

commit v1 on v0

--- a/solution.py
+++ b/solution.py
@@ -96,7 +96,7 @@
     local_gram = jnp.einsum(
         "arn,brn->nab", basis_stack, basis_stack, precision=lax.Precision.HIGHEST
     )
-    gram_matrix = lax.psum(local_gram, "dom")
+    gram_matrix = jnp.sum(lax.all_gather(local_gram, "dom"), axis=0)
     point_c, resid_c, direc_c = coefficient_steps(gram_matrix)
     highest = lax.Precision.HIGHEST
     new_point = start_point + jnp.einsum("na,arn->rn", point_c, basis_stack, precision=highest)

time: 523 us -> 456 us (0.87)
  waiting for transfers between devices: 151 us -> 82.4 us
  local copies, waits for them, and re-layouts: 95.6 us -> 101 us
    psum x1 -> x0, waiting for transfers between devices: 135 us -> none  [shards(): gram_matrix = lax.psum(local_gram, 'dom')]
    all_gather x0 -> x1, waiting for transfers between devices: none -> 67.1 us  [shards(): gram_matrix = jnp.sum(lax.all_gather(local_gram, 'dom'), axis=0)]
    unnamed x13 -> x1, other arithmetic: 10.1 us -> 4.24 us
  transfers between devices with their start and end apart: 45 -> 45, of which waited for: 7 -> 8; matrix products, arithmetic and copies ran while one was open for 18% -> 21% of each run, Pallas kernels for 0% -> 0%
where the time goes in v1:
time: 456 us; the launch traced here: 449 us
  starting transfers between devices  118 us (26%)
  matrix products  117 us (26%)
  local copies, waits for them, and re-layouts  101 us (22%)
  waiting for transfers between devices  82.4 us (18%)
  between operations  16.5 us (4%)
  other arithmetic  13.1 us (3%)
    ppermute x44, starting transfers between devices, from_behind(): lax.ppermute(shard, axis, [(i, (i + by) % peers) for i in range(peers)])  118 us
    all_gather x1, waiting for transfers between devices, shards(): gram_matrix = jnp.sum(lax.all_gather(local_gram, 'dom'), axis=0)  67.1 us
    concatenate x11, local copies, waits for them, and re-layouts, apply_blocks(): ghost_table = jnp.concatenate(pieces, axis=0)  63.7 us
    dot_general x44, matrix products, apply_blocks(): outgoing = jnp.dot(chooser, flat_rows, precision=highest)  45.3 us
    dot_general x66, matrix products, apply_blocks(): jnp.dot(chooser, ghost_table, precision=highest)  36.4 us
    dot_general x66, matrix products, apply_blocks(): jnp.einsum('icb,ibw->icw', block_vals[:, slot_index], picked, precision=h...  25.3 us
    another operation x14, local copies, waits for them, and re-layouts, shards(): basis_stack = jnp.stack(p_basis + r_basis)  19 us
    ppermute x44, waiting for transfers between devices, from_behind(): lax.ppermute(shard, axis, [(i, (i + by) % peers) for i in range(peers)])  15.3 us
  transfers between devices with their start and end apart: 45, of which 8 were waited for; matrix products, arithmetic and copies ran while one was open for 21% of the time, Pallas kernels for 0%

profile of v1, /device:TPU:0, one launch (start us, length us, event | category | flops | bytes accessed | tf_op | source)
XLA Modules:
  0.0 448.7 jit_solution(2974008798314820287)
XLA Ops:
  7.2 1.2 slice_reduce_fusion.6
  9.9 6.5 %collective-permute-start.24 = (f32[3,16384]{1,0:T(4,128)S(1)}, f32[3,16384]{1,0:T(4,128)S(1)}, u32[]{:S(2)}, u32[]{:S(2)}) collective-permute-start(f32[3,16384]{1,0:T(4,128)S(1)} %fusion.361), channel_id=1, source_target_pairs={{0,31},{1,0},{2,1},{3,2},{4,3},{5,4},{6,5},{7,6},{8,7},{9,8},{10,9... | collective-permute-start | bytes 589832 | tf_op jit(solution)/shard_map/ppermute | solution.py:14
  18.6 1.3 collective-permute-start.27
  21.1 5.0 %collective-permute-start = (f32[3,16384]{1,0:T(4,128)}, f32[3,16384]{1,0:T(4,128)}, u32[]{:S(2)}, u32[]{:S(2)}) collective-permute-start(f32[3,16384]{1,0:T(4,128)} %fusion.367), channel_id=1, source_target_pairs={{0,31},{1,0},{2,1},{3,2},{4,3},{5,4},{6,5},{7,6},{8,7},{9,8},{10,9... | collective-permute-start | bytes 589832 | tf_op jit(solution)/shard_map/ppermute | solution.py:14
  32.4 8.0 %collective-permute-start.3 = (f32[3,16384]{1,0:T(4,128)}, f32[3,16384]{1,0:T(4,128)}, u32[]{:S(2)}, u32[]{:S(2)}) collective-permute-start(f32[3,16384]{1,0:T(4,128)} %fusion.334), channel_id=1, source_target_pairs={{0,2},{1,3},{2,4},{3,5},{4,6},{5,7},{6,8},{7,9},{8,10},{9,11},{10,... | collective-permute-start | bytes 589832 | tf_op jit(solution)/shard_map/ppermute | solution.py:14
  40.3 2.2 concatenate.39
  54.0 6.4 %concatenate.33 = f32[16,16384]{1,0:T(8,128)S(1)} concatenate(f32[4,16384]{1,0:T(4,128)S(1)} %reshape_reshape.33, f32[3,16384]{1,0:T(4,128)} %collective-permute-done, f32[3,16384]{1,0:T(4,128)} %collective-permute-done.1, f32[3,16384]{1,0:T(4,128)} %collective-permute-done.2, f32[3,16384]{1,0:T(4,128)} %collective-permute-done.3), dimensions={0} | concatenate | bytes 2097152 | tf_op jit(solution)/shard_map/concatenate | solution.py:29
  70.2 2.6 collective-permute-start.28
  72.9 1.9 collective-permute-start.31
  74.8 5.1 %collective-permute-start.4 = (f32[3,16384]{1,0:T(4,128)}, f32[3,16384]{1,0:T(4,128)}, u32[]{:S(2)}, u32[]{:S(2)}) collective-permute-start(f32[3,16384]{1,0:T(4,128)} %fusion.366), channel_id=1, source_target_pairs={{0,31},{1,0},{2,1},{3,2},{4,3},{5,4},{6,5},{7,6},{8,7},{9,8},{10,9... | collective-permute-start | bytes 589832 | tf_op jit(solution)/shard_map/ppermute | solution.py:14
  82.9 1.9 collective-permute-start.5
  84.9 12.7 %collective-permute-start.7 = (f32[3,16384]{1,0:T(4,128)}, f32[3,16384]{1,0:T(4,128)}, u32[]{:S(2)}, u32[]{:S(2)}) collective-permute-start(f32[3,16384]{1,0:T(4,128)} %fusion.333), channel_id=1, source_target_pairs={{0,2},{1,3},{2,4},{3,5},{4,6},{5,7},{6,8},{7,9},{8,10},{9,11},{10,... | collective-permute-start | bytes 589832 | tf_op jit(solution)/shard_map/ppermute | solution.py:14
  97.7 6.5 %concatenate.40 = f32[16,16384]{1,0:T(8,128)S(1)} concatenate(f32[4,16384]{1,0:T(4,128)S(1)} %reshape_reshape.40, f32[3,16384]{1,0:T(4,128)} %copy-done.36, f32[3,16384]{1,0:T(4,128)} %copy-done.39, f32[3,16384]{1,0:T(4,128)} %copy-done.42, f32[3,16384]{1,0:T(4,128)} %collective-permute-done.31), dimensions={0} | concatenate | bytes 2097152 | tf_op jit(solution)/shard_map/concatenate | solution.py:29
  114.6 6.7 %concatenate.34 = f32[16,16384]{1,0:T(8,128)S(1)} concatenate(f32[4,16384]{1,0:T(4,128)S(1)} %reshape_reshape.34, f32[3,16384]{1,0:T(4,128)} %collective-permute-done.4, f32[3,16384]{1,0:T(4,128)} %collective-permute-done.5, f32[3,16384]{1,0:T(4,128)} %collective-permute-done.6, f32[3,16384]{1,0:T(4,128)} %collective-permute-done.7), dimensions={0} | concatenate | bytes 2097152 | tf_op jit(solution)/shard_map/concatenate | solution.py:29
  132.3 1.8 collective-permute-start.34
  134.3 4.8 %collective-permute-start.32 = (f32[3,16384]{1,0:T(4,128)S(1)}, f32[3,16384]{1,0:T(4,128)}, u32[]{:S(2)}, u32[]{:S(2)}) collective-permute-start(f32[3,16384]{1,0:T(4,128)S(1)} %fusion.359), channel_id=1, source_target_pairs={{0,31},{1,0},{2,1},{3,2},{4,3},{5,4},{6,5},{7,6},{8,7},{9,8},{10,9... | collective-permute-start | bytes 589832 | tf_op jit(solution)/shard_map/ppermute | solution.py:14
  140.8 1.4 collective-permute-done.34
  142.2 10.1 %collective-permute-start.9 = (f32[3,16384]{1,0:T(4,128)}, f32[3,16384]{1,0:T(4,128)}, u32[]{:S(2)}, u32[]{:S(2)}) collective-permute-start(f32[3,16384]{1,0:T(4,128)} %fusion.354), channel_id=1, source_target_pairs={{0,30},{1,31},{2,0},{3,1},{4,2},{5,3},{6,4},{7,5},{8,6},{9,7},{10,... | collective-permute-start | bytes 589832 | tf_op jit(solution)/shard_map/ppermute | solution.py:14
  152.3 5.4 %collective-permute-start.8 = (f32[3,16384]{1,0:T(4,128)}, f32[3,16384]{1,0:T(4,128)}, u32[]{:S(2)}, u32[]{:S(2)}) collective-permute-start(f32[3,16384]{1,0:T(4,128)} %fusion.365), channel_id=1, source_target_pairs={{0,31},{1,0},{2,1},{3,2},{4,3},{5,4},{6,5},{7,6},{8,7},{9,8},{10,9... | collective-permute-start | bytes 589832 | tf_op jit(solution)/shard_map/ppermute | solution.py:14
  157.8 3.3 concatenate.41
  172.2 6.4 %concatenate.35 = f32[16,16384]{1,0:T(8,128)S(1)} concatenate(f32[4,16384]{1,0:T(4,128)S(1)} %reshape_reshape.35, f32[3,16384]{1,0:T(4,128)} %collective-permute-done.8, f32[3,16384]{1,0:T(4,128)} %collective-permute-done.9, f32[3,16384]{1,0:T(4,128)} %collective-permute-done.10, f32[3,16384]{1,0:T(4,128)} %collective-permute-done.11), dimensions={0} | concatenate | bytes 2097152 | tf_op jit(solution)/shard_map/concatenate | solution.py:29
  189.6 3.5 collective-permute-start.38
  193.1 2.6 collective-permute-start.39
  196.7 4.1 collective-permute-start.12
  203.0 4.5 collective-permute-done.37
  207.5 6.5 %collective-permute-start.15 = (f32[3,16384]{1,0:T(4,128)}, f32[3,16384]{1,0:T(4,128)}, u32[]{:S(2)}, u32[]{:S(2)}) collective-permute-start(f32[3,16384]{1,0:T(4,128)} %fusion.331), channel_id=1, source_target_pairs={{0,2},{1,3},{2,4},{3,5},{4,6},{5,7},{6,8},{7,9},{8,10},{9,11},{10,... | collective-permute-start | bytes 589832 | tf_op jit(solution)/shard_map/ppermute | solution.py:14
  214.0 6.5 %concatenate.42 = f32[16,16384]{1,0:T(8,128)S(1)} concatenate(f32[4,16384]{1,0:T(4,128)S(1)} %reshape_reshape.42, f32[3,16384]{1,0:T(4,128)} %copy-done.37, f32[3,16384]{1,0:T(4,128)} %copy-done.40, f32[3,16384]{1,0:T(4,128)} %copy-done.43, f32[3,16384]{1,0:T(4,128)} %collective-permute-done.39), dimensions={0} | concatenate | bytes 2097152 | tf_op jit(solution)/shard_map/concatenate | solution.py:29
  231.6 6.7 %concatenate.36 = f32[16,16384]{1,0:T(8,128)S(1)} concatenate(f32[4,16384]{1,0:T(4,128)S(1)} %reshape_reshape.36, f32[3,16384]{1,0:T(4,128)} %collective-permute-done.12, f32[3,16384]{1,0:T(4,128)} %collective-permute-done.13, f32[3,16384]{1,0:T(4,128)} %collective-permute-done.14, f32[3,16384]{1,0:T(4,128)} %collective-permute-done.15), dimensions={0} | concatenate | bytes 2097152 | tf_op jit(solution)/shard_map/concatenate | solution.py:29
  247.5 2.7 collective-permute-start.40
  250.6 1.6 collective-permute-start.43
  253.2 5.1 %collective-permute-start.16 = (f32[3,16384]{1,0:T(4,128)}, f32[3,16384]{1,0:T(4,128)}, u32[]{:S(2)}, u32[]{:S(2)}) collective-permute-start(f32[3,16384]{1,0:T(4,128)} %fusion.363), channel_id=1, source_target_pairs={{0,31},{1,0},{2,1},{3,2},{4,3},{5,4},{6,5},{7,6},{8,7},{9,8},{10,9... | collective-permute-start | bytes 589832 | tf_op jit(solution)/shard_map/ppermute | solution.py:14
  260.4 1.5 collective-permute-start.17
  263.0 14.1 %collective-permute-start.19 = (f32[3,16384]{1,0:T(4,128)}, f32[3,16384]{1,0:T(4,128)}, u32[]{:S(2)}, u32[]{:S(2)}) collective-permute-start(f32[3,16384]{1,0:T(4,128)} %fusion.330), channel_id=1, source_target_pairs={{0,2},{1,3},{2,4},{3,5},{4,6},{5,7},{6,8},{7,9},{8,10},{9,11},{10,... | collective-permute-start | bytes 589832 | tf_op jit(solution)/shard_map/ppermute | solution.py:14
  277.1 6.2 %concatenate.43 = f32[16,16384]{1,0:T(8,128)S(1)} concatenate(f32[4,16384]{1,0:T(4,128)S(1)} %reshape_reshape.43, f32[3,16384]{1,0:T(4,128)} %copy-done.38, f32[3,16384]{1,0:T(4,128)} %copy-done.41, f32[3,16384]{1,0:T(4,128)} %copy-done.44, f32[3,16384]{1,0:T(4,128)} %collective-permute-done.43), dimensions={0} | concatenate | bytes 2097152 | tf_op jit(solution)/shard_map/concatenate | solution.py:29
  284.5 1.2 convolution_bitcast_fusion.4
  289.2 1.2 convolution_bitcast_fusion
  290.5 6.4 %concatenate.37 = f32[16,16384]{1,0:T(8,128)S(1)} concatenate(f32[4,16384]{1,0:T(4,128)S(1)} %reshape_reshape.37, f32[3,16384]{1,0:T(4,128)} %collective-permute-done.16, f32[3,16384]{1,0:T(4,128)} %collective-permute-done.17, f32[3,16384]{1,0:T(4,128)} %collective-permute-done.18, f32[3,16384]{1,0:T(4,128)} %collective-permute-done.19), dimensions={0} | concatenate | bytes 2097152 | tf_op jit(solution)/shard_map/concatenate | solution.py:29
  309.1 2.7 collective-permute-start.20
  312.0 1.8 collective-permute-start.23
  316.0 2.3 collective-permute-done.20
  318.3 5.8 %collective-permute-done.21 = f32[3,16384]{1,0:T(4,128)S(1)} collective-permute-done((f32[3,16384]{1,0:T(4,128)}, f32[3,16384]{1,0:T(4,128)S(1)}, u32[]{:S(2)}, u32[]{:S(2)}) %collective-permute-start.21) | collective-permute-done | bytes 196640 | tf_op jit(solution)/shard_map/ppermute | solution.py:14
  325.5 6.4 %concatenate.38 = f32[16,16384]{1,0:T(8,128)S(1)} concatenate(f32[4,16384]{1,0:T(4,128)S(1)} %reshape_reshape.38, f32[3,16384]{1,0:T(4,128)} %copy-done.46, f32[3,16384]{1,0:T(4,128)} %copy-done.48, f32[3,16384]{1,0:T(4,128)} %copy-done.49, f32[3,16384]{1,0:T(4,128)} %collective-permute-done.23), dimensions={0} | concatenate | bytes 2097152 | tf_op jit(solution)/shard_map/concatenate | solution.py:29
  339.0 8.8 %stack.55 = f32[13,512,128]{1,0,2:T(8,128)} concatenate(f32[1,512,128]{1,0,2:T(1,128)S(1)} %copy-done.25, f32[1,512,128]{1,0,2:T(1,128)S(1)} %copy-done.28, f32[1,512,128]{1,0,2:T(1,128)S(1)} %copy-done.30, f32[1,512,128]{1,0,2:T(1,128)S(1)} %copy-done.32, f32[1,512,128]{1,0,2:T(1,128)S(1)} %copy-done.34, f32[1,512,128]{1,0,2:T(1,128)S(1)} %copy.155, f32[1,512,128]{1,0,2:T(1,128)S(1)} %copy.156, ...), dimensions={0} | concatenate | bytes 6815744 | tf_op jit(solution)/shard_map/stack | solution.py:95
  347.8 9.0 %fusion.499 = f32[128,13,13]{2,1,0:T(8,128)S(1)} fusion(f32[13,512,128]{1,0,2:T(8,128)} %stack.55), kind=kOutput, calls=%fused_computation.689 | convolution fusion | flops 132907008 | bytes 3494400 | tf_op jit(solution)/shard_map/arn,brn->nab/dot_general | solution.py:96
  358.1 67.1 %all-gather.3.cloned.1.call-done = f32[4096,13,13]{0,2,1:T(8,128)} async-done(((f32[128,13,13]{0,2,1:T(8,128)}), f32[4096,13,13]{0,2,1:T(8,128)}) %all-gather.3.cloned.1.call-update) | async-done | bytes 2768912 | tf_op jit(solution)/shard_map/all_gather | solution.py:99
  425.2 4.6 %reshape.408 = f32[32,128,13,13]{1,0,3,2:T(8,128)} reshape(f32[4096,13,13]{0,2,1:T(8,128)} %all-gather.3.cloned.1.call-done) | data formatting | bytes 5537792 | tf_op jit(solution)/shard_map/all_gather | solution.py:99
  429.8 2.2 reduce_sum.121
  434.7 4.2 multiply_reduce_fusion
  (467 shorter events, 141.6 us)
Async XLA Ops:
  7.2 418.0 %all-gather.3.cloned.1.call-start = ((), (), s32[]{:S(2)}) async-start(), calls=%async_computation | async-start | bytes 3514368 | tf_op jit(solution)/shard_map/all_gather | solution.py:99
  9.9 21.8 %collective-permute-start.24 = (f32[3,16384]{1,0:T(4,128)S(1)}, f32[3,16384]{1,0:T(4,128)S(1)}, u32[]{:S(2)}, u32[]{:S(2)}) collective-permute-start(f32[3,16384]{1,0:T(4,128)S(1)} %fusion.361), channel_id=1, source_target_pairs={{0,31},{1,0},{2,1},{3,2},{4,3},{5,4},{6,5},{7,6},{8,7},{9,8},{10,9... | collective-permute-start | bytes 589832 | tf_op jit(solution)/shard_map/ppermute | solution.py:14
  16.8 15.5 %collective-permute-start.25 = (f32[3,16384]{1,0:T(4,128)S(1)}, f32[3,16384]{1,0:T(4,128)S(1)}, u32[]{:S(2)}, u32[]{:S(2)}) collective-permute-start(f32[3,16384]{1,0:T(4,128)S(1)} %fusion.350), channel_id=1, source_target_pairs={{0,30},{1,31},{2,0},{3,1},{4,2},{5,3},{6,4},{7,5},{8,6},{9,7},{10,... | collective-permute-start | bytes 589832 | tf_op jit(solution)/shard_map/ppermute | solution.py:14
  17.9 14.5 %collective-permute-start.26 = (f32[3,16384]{1,0:T(4,128)S(1)}, f32[3,16384]{1,0:T(4,128)S(1)}, u32[]{:S(2)}, u32[]{:S(2)}) collective-permute-start(f32[3,16384]{1,0:T(4,128)S(1)} %fusion.339), channel_id=1, source_target_pairs={{0,1},{1,2},{2,3},{3,4},{4,5},{5,6},{6,7},{7,8},{8,9},{9,10},{10,1... | collective-permute-start | bytes 589832 | tf_op jit(solution)/shard_map/ppermute | solution.py:14
  18.6 21.8 %collective-permute-start.27 = (f32[3,16384]{1,0:T(4,128)S(1)}, f32[3,16384]{1,0:T(4,128)}, u32[]{:S(2)}, u32[]{:S(2)}) collective-permute-start(f32[3,16384]{1,0:T(4,128)S(1)} %fusion.328), channel_id=1, source_target_pairs={{0,2},{1,3},{2,4},{3,5},{4,6},{5,7},{6,8},{7,9},{8,10},{9,11},{10,... | collective-permute-start | bytes 589832 | tf_op jit(solution)/shard_map/ppermute | solution.py:14
  21.1 32.8 %collective-permute-start = (f32[3,16384]{1,0:T(4,128)}, f32[3,16384]{1,0:T(4,128)}, u32[]{:S(2)}, u32[]{:S(2)}) collective-permute-start(f32[3,16384]{1,0:T(4,128)} %fusion.367), channel_id=1, source_target_pairs={{0,31},{1,0},{2,1},{3,2},{4,3},{5,4},{6,5},{7,6},{8,7},{9,8},{10,9... | collective-permute-start | bytes 589832 | tf_op jit(solution)/shard_map/ppermute | solution.py:14
  26.3 22.2 %copy-start.3 = (f32[512,128]{0,1:T(8,128)}, f32[512,128]{0,1:T(8,128)S(1)}, u32[]{:S(2)}) copy-start(f32[512,128]{0,1:T(8,128)S(1)} %copy.141) | copy-start | bytes 786436
  28.7 37.2 %copy-start.1 = (f32[512,128]{0,1:T(8,128)}, f32[512,128]{0,1:T(8,128)S(1)}, u32[]{:S(2)}) copy-start(f32[512,128]{0,1:T(8,128)S(1)} %copy.128) | copy-start | bytes 786436
  31.8 22.2 %collective-permute-start.1 = (f32[3,16384]{1,0:T(4,128)}, f32[3,16384]{1,0:T(4,128)}, u32[]{:S(2)}, u32[]{:S(2)}) collective-permute-start(f32[3,16384]{1,0:T(4,128)} %fusion.356), channel_id=1, source_target_pairs={{0,30},{1,31},{2,0},{3,1},{4,2},{5,3},{6,4},{7,5},{8,6},{9,7},{10,... | collective-permute-start | bytes 589832 | tf_op jit(solution)/shard_map/ppermute | solution.py:14
  32.3 21.6 %collective-permute-start.2 = (f32[3,16384]{1,0:T(4,128)}, f32[3,16384]{1,0:T(4,128)}, u32[]{:S(2)}, u32[]{:S(2)}) collective-permute-start(f32[3,16384]{1,0:T(4,128)} %fusion.345), channel_id=1, source_target_pairs={{0,1},{1,2},{2,3},{3,4},{4,5},{5,6},{6,7},{7,8},{8,9},{9,10},{10,1... | collective-permute-start | bytes 589832 | tf_op jit(solution)/shard_map/ppermute | solution.py:14
  32.4 21.6 %collective-permute-start.3 = (f32[3,16384]{1,0:T(4,128)}, f32[3,16384]{1,0:T(4,128)}, u32[]{:S(2)}, u32[]{:S(2)}) collective-permute-start(f32[3,16384]{1,0:T(4,128)} %fusion.334), channel_id=1, source_target_pairs={{0,2},{1,3},{2,4},{3,5},{4,6},{5,7},{6,8},{7,9},{8,10},{9,11},{10,... | collective-permute-start | bytes 589832 | tf_op jit(solution)/shard_map/ppermute | solution.py:14
  70.2 12.7 %collective-permute-start.28 = (f32[3,16384]{1,0:T(4,128)}, f32[3,16384]{1,0:T(4,128)S(1)}, u32[]{:S(2)}, u32[]{:S(2)}) collective-permute-start(f32[3,16384]{1,0:T(4,128)} %fusion.360), channel_id=1, source_target_pairs={{0,31},{1,0},{2,1},{3,2},{4,3},{5,4},{6,5},{7,6},{8,7},{9,8},{10,9... | collective-permute-start | bytes 589832 | tf_op jit(solution)/shard_map/ppermute | solution.py:14
  72.8 12.1 %collective-permute-start.29 = (f32[3,16384]{1,0:T(4,128)}, f32[3,16384]{1,0:T(4,128)S(1)}, u32[]{:S(2)}, u32[]{:S(2)}) collective-permute-start(f32[3,16384]{1,0:T(4,128)} %fusion.349), channel_id=1, source_target_pairs={{0,30},{1,31},{2,0},{3,1},{4,2},{5,3},{6,4},{7,5},{8,6},{9,7},{10,... | collective-permute-start | bytes 589832 | tf_op jit(solution)/shard_map/ppermute | solution.py:14
  72.8 12.1 %collective-permute-start.30 = (f32[3,16384]{1,0:T(4,128)}, f32[3,16384]{1,0:T(4,128)S(1)}, u32[]{:S(2)}, u32[]{:S(2)}) collective-permute-start(f32[3,16384]{1,0:T(4,128)} %fusion.338), channel_id=1, source_target_pairs={{0,1},{1,2},{2,3},{3,4},{4,5},{5,6},{6,7},{7,8},{8,9},{9,10},{10,1... | collective-permute-start | bytes 589832 | tf_op jit(solution)/shard_map/ppermute | solution.py:14
  72.9 24.8 %collective-permute-start.31 = (f32[3,16384]{1,0:T(4,128)S(1)}, f32[3,16384]{1,0:T(4,128)}, u32[]{:S(2)}, u32[]{:S(2)}) collective-permute-start(f32[3,16384]{1,0:T(4,128)S(1)} %copy-done.50), channel_id=1, source_target_pairs={{0,2},{1,3},{2,4},{3,5},{4,6},{5,7},{6,8},{7,9},{8,10},{9,11},{10,... | collective-permute-start | bytes 589832 | tf_op jit(solution)/shard_map/ppermute | solution.py:14
  74.8 39.7 %collective-permute-start.4 = (f32[3,16384]{1,0:T(4,128)}, f32[3,16384]{1,0:T(4,128)}, u32[]{:S(2)}, u32[]{:S(2)}) collective-permute-start(f32[3,16384]{1,0:T(4,128)} %fusion.366), channel_id=1, source_target_pairs={{0,31},{1,0},{2,1},{3,2},{4,3},{5,4},{6,5},{7,6},{8,7},{9,8},{10,9... | collective-permute-start | bytes 589832 | tf_op jit(solution)/shard_map/ppermute | solution.py:14
  82.9 31.6 %collective-permute-start.5 = (f32[3,16384]{1,0:T(4,128)}, f32[3,16384]{1,0:T(4,128)}, u32[]{:S(2)}, u32[]{:S(2)}) collective-permute-start(f32[3,16384]{1,0:T(4,128)} %fusion.355), channel_id=1, source_target_pairs={{0,30},{1,31},{2,0},{3,1},{4,2},{5,3},{6,4},{7,5},{8,6},{9,7},{10,... | collective-permute-start | bytes 589832 | tf_op jit(solution)/shard_map/ppermute | solution.py:14
  84.9 29.6 %collective-permute-start.6 = (f32[3,16384]{1,0:T(4,128)}, f32[3,16384]{1,0:T(4,128)}, u32[]{:S(2)}, u32[]{:S(2)}) collective-permute-start(f32[3,16384]{1,0:T(4,128)} %fusion.344), channel_id=1, source_target_pairs={{0,1},{1,2},{2,3},{3,4},{4,5},{5,6},{6,7},{7,8},{8,9},{9,10},{10,1... | collective-permute-start | bytes 589832 | tf_op jit(solution)/shard_map/ppermute | solution.py:14
  84.9 29.6 %collective-permute-start.7 = (f32[3,16384]{1,0:T(4,128)}, f32[3,16384]{1,0:T(4,128)}, u32[]{:S(2)}, u32[]{:S(2)}) collective-permute-start(f32[3,16384]{1,0:T(4,128)} %fusion.333), channel_id=1, source_target_pairs={{0,2},{1,3},{2,4},{3,5},{4,6},{5,7},{6,8},{7,9},{8,10},{9,11},{10,... | collective-permute-start | bytes 589832 | tf_op jit(solution)/shard_map/ppermute | solution.py:14
  131.2 9.1 %collective-permute-start.33 = (f32[3,16384]{1,0:T(4,128)}, f32[3,16384]{1,0:T(4,128)S(1)}, u32[]{:S(2)}, u32[]{:S(2)}) collective-permute-start(f32[3,16384]{1,0:T(4,128)} %fusion.348), channel_id=1, source_target_pairs={{0,30},{1,31},{2,0},{3,1},{4,2},{5,3},{6,4},{7,5},{8,6},{9,7},{10,... | collective-permute-start | bytes 589832 | tf_op jit(solution)/shard_map/ppermute | solution.py:14
  132.3 9.9 %collective-permute-start.34 = (f32[3,16384]{1,0:T(4,128)S(1)}, f32[3,16384]{1,0:T(4,128)S(1)}, u32[]{:S(2)}, u32[]{:S(2)}) collective-permute-start(f32[3,16384]{1,0:T(4,128)S(1)} %copy-done.52), channel_id=1, source_target_pairs={{0,1},{1,2},{2,3},{3,4},{4,5},{5,6},{6,7},{7,8},{8,9},{9,10},{10,1... | collective-permute-start | bytes 589832 | tf_op jit(solution)/shard_map/ppermute | solution.py:14
  134.0 18.3 %collective-permute-start.35 = (f32[3,16384]{1,0:T(4,128)S(1)}, f32[3,16384]{1,0:T(4,128)S(1)}, u32[]{:S(2)}, u32[]{:S(2)}) collective-permute-start(f32[3,16384]{1,0:T(4,128)S(1)} %copy-done.51), channel_id=1, source_target_pairs={{0,2},{1,3},{2,4},{3,5},{4,6},{5,7},{6,8},{7,9},{8,10},{9,11},{10,... | collective-permute-start | bytes 589832 | tf_op jit(solution)/shard_map/ppermute | solution.py:14
  134.3 23.5 %collective-permute-start.32 = (f32[3,16384]{1,0:T(4,128)S(1)}, f32[3,16384]{1,0:T(4,128)}, u32[]{:S(2)}, u32[]{:S(2)}) collective-permute-start(f32[3,16384]{1,0:T(4,128)S(1)} %fusion.359), channel_id=1, source_target_pairs={{0,31},{1,0},{2,1},{3,2},{4,3},{5,4},{6,5},{7,6},{8,7},{9,8},{10,9... | collective-permute-start | bytes 589832 | tf_op jit(solution)/shard_map/ppermute | solution.py:14
  139.0 33.2 %collective-permute-start.10 = (f32[3,16384]{1,0:T(4,128)}, f32[3,16384]{1,0:T(4,128)}, u32[]{:S(2)}, u32[]{:S(2)}) collective-permute-start(f32[3,16384]{1,0:T(4,128)} %fusion.343), channel_id=1, source_target_pairs={{0,1},{1,2},{2,3},{3,4},{4,5},{5,6},{6,7},{7,8},{8,9},{9,10},{10,1... | collective-permute-start | bytes 589832 | tf_op jit(solution)/shard_map/ppermute | solution.py:14
  140.3 31.9 %collective-permute-start.11 = (f32[3,16384]{1,0:T(4,128)}, f32[3,16384]{1,0:T(4,128)}, u32[]{:S(2)}, u32[]{:S(2)}) collective-permute-start(f32[3,16384]{1,0:T(4,128)} %fusion.332), channel_id=1, source_target_pairs={{0,2},{1,3},{2,4},{3,5},{4,6},{5,7},{6,8},{7,9},{8,10},{9,11},{10,... | collective-permute-start | bytes 589832 | tf_op jit(solution)/shard_map/ppermute | solution.py:14
  142.2 30.0 %collective-permute-start.9 = (f32[3,16384]{1,0:T(4,128)}, f32[3,16384]{1,0:T(4,128)}, u32[]{:S(2)}, u32[]{:S(2)}) collective-permute-start(f32[3,16384]{1,0:T(4,128)} %fusion.354), channel_id=1, source_target_pairs={{0,30},{1,31},{2,0},{3,1},{4,2},{5,3},{6,4},{7,5},{8,6},{9,7},{10,... | collective-permute-start | bytes 589832 | tf_op jit(solution)/shard_map/ppermute | solution.py:14
  152.3 19.9 %collective-permute-start.8 = (f32[3,16384]{1,0:T(4,128)}, f32[3,16384]{1,0:T(4,128)}, u32[]{:S(2)}, u32[]{:S(2)}) collective-permute-start(f32[3,16384]{1,0:T(4,128)} %fusion.365), channel_id=1, source_target_pairs={{0,31},{1,0},{2,1},{3,2},{4,3},{5,4},{6,5},{7,6},{8,7},{9,8},{10,9... | collective-permute-start | bytes 589832 | tf_op jit(solution)/shard_map/ppermute | solution.py:14
  188.6 14.3 %collective-permute-start.36 = (f32[3,16384]{1,0:T(4,128)}, f32[3,16384]{1,0:T(4,128)S(1)}, u32[]{:S(2)}, u32[]{:S(2)}) collective-permute-start(f32[3,16384]{1,0:T(4,128)} %fusion.358), channel_id=1, source_target_pairs={{0,31},{1,0},{2,1},{3,2},{4,3},{5,4},{6,5},{7,6},{8,7},{9,8},{10,9... | collective-permute-start | bytes 589832 | tf_op jit(solution)/shard_map/ppermute | solution.py:14
  189.3 18.2 %collective-permute-start.37 = (f32[3,16384]{1,0:T(4,128)}, f32[3,16384]{1,0:T(4,128)S(1)}, u32[]{:S(2)}, u32[]{:S(2)}) collective-permute-start(f32[3,16384]{1,0:T(4,128)} %fusion.347), channel_id=1, source_target_pairs={{0,30},{1,31},{2,0},{3,1},{4,2},{5,3},{6,4},{7,5},{8,6},{9,7},{10,... | collective-permute-start | bytes 589832 | tf_op jit(solution)/shard_map/ppermute | solution.py:14
  189.6 17.9 %collective-permute-start.38 = (f32[3,16384]{1,0:T(4,128)}, f32[3,16384]{1,0:T(4,128)S(1)}, u32[]{:S(2)}, u32[]{:S(2)}) collective-permute-start(f32[3,16384]{1,0:T(4,128)} %fusion.336), channel_id=1, source_target_pairs={{0,1},{1,2},{2,3},{3,4},{4,5},{5,6},{6,7},{7,8},{8,9},{9,10},{10,1... | collective-permute-start | bytes 589832 | tf_op jit(solution)/shard_map/ppermute | solution.py:14
  193.1 20.8 %collective-permute-start.39 = (f32[3,16384]{1,0:T(4,128)}, f32[3,16384]{1,0:T(4,128)}, u32[]{:S(2)}, u32[]{:S(2)}) collective-permute-start(f32[3,16384]{1,0:T(4,128)} %fusion.325), channel_id=1, source_target_pairs={{0,2},{1,3},{2,4},{3,5},{4,6},{5,7},{6,8},{7,9},{8,10},{9,11},{10,... | collective-permute-start | bytes 589832 | tf_op jit(solution)/shard_map/ppermute | solution.py:14
  196.7 34.9 %collective-permute-start.12 = (f32[3,16384]{1,0:T(4,128)}, f32[3,16384]{1,0:T(4,128)}, u32[]{:S(2)}, u32[]{:S(2)}) collective-permute-start(f32[3,16384]{1,0:T(4,128)} %fusion.364), channel_id=1, source_target_pairs={{0,31},{1,0},{2,1},{3,2},{4,3},{5,4},{6,5},{7,6},{8,7},{9,8},{10,9... | collective-permute-start | bytes 589832 | tf_op jit(solution)/shard_map/ppermute | solution.py:14
  202.9 28.7 %collective-permute-start.13 = (f32[3,16384]{1,0:T(4,128)}, f32[3,16384]{1,0:T(4,128)}, u32[]{:S(2)}, u32[]{:S(2)}) collective-permute-start(f32[3,16384]{1,0:T(4,128)} %fusion.353), channel_id=1, source_target_pairs={{0,30},{1,31},{2,0},{3,1},{4,2},{5,3},{6,4},{7,5},{8,6},{9,7},{10,... | collective-permute-start | bytes 589832 | tf_op jit(solution)/shard_map/ppermute | solution.py:14
  207.4 24.1 %collective-permute-start.14 = (f32[3,16384]{1,0:T(4,128)}, f32[3,16384]{1,0:T(4,128)}, u32[]{:S(2)}, u32[]{:S(2)}) collective-permute-start(f32[3,16384]{1,0:T(4,128)} %fusion.342), channel_id=1, source_target_pairs={{0,1},{1,2},{2,3},{3,4},{4,5},{5,6},{6,7},{7,8},{8,9},{9,10},{10,1... | collective-permute-start | bytes 589832 | tf_op jit(solution)/shard_map/ppermute | solution.py:14
  207.5 24.1 %collective-permute-start.15 = (f32[3,16384]{1,0:T(4,128)}, f32[3,16384]{1,0:T(4,128)}, u32[]{:S(2)}, u32[]{:S(2)}) collective-permute-start(f32[3,16384]{1,0:T(4,128)} %fusion.331), channel_id=1, source_target_pairs={{0,2},{1,3},{2,4},{3,5},{4,6},{5,7},{6,8},{7,9},{8,10},{9,11},{10,... | collective-permute-start | bytes 589832 | tf_op jit(solution)/shard_map/ppermute | solution.py:14
  247.5 12.9 %collective-permute-start.40 = (f32[3,16384]{1,0:T(4,128)}, f32[3,16384]{1,0:T(4,128)S(1)}, u32[]{:S(2)}, u32[]{:S(2)}) collective-permute-start(f32[3,16384]{1,0:T(4,128)} %fusion.357), channel_id=1, source_target_pairs={{0,31},{1,0},{2,1},{3,2},{4,3},{5,4},{6,5},{7,6},{8,7},{9,8},{10,9... | collective-permute-start | bytes 589832 | tf_op jit(solution)/shard_map/ppermute | solution.py:14
  250.2 12.8 %collective-permute-start.41 = (f32[3,16384]{1,0:T(4,128)}, f32[3,16384]{1,0:T(4,128)S(1)}, u32[]{:S(2)}, u32[]{:S(2)}) collective-permute-start(f32[3,16384]{1,0:T(4,128)} %fusion.346), channel_id=1, source_target_pairs={{0,30},{1,31},{2,0},{3,1},{4,2},{5,3},{6,4},{7,5},{8,6},{9,7},{10,... | collective-permute-start | bytes 589832 | tf_op jit(solution)/shard_map/ppermute | solution.py:14
  250.4 12.6 %collective-permute-start.42 = (f32[3,16384]{1,0:T(4,128)}, f32[3,16384]{1,0:T(4,128)S(1)}, u32[]{:S(2)}, u32[]{:S(2)}) collective-permute-start(f32[3,16384]{1,0:T(4,128)} %fusion.335), channel_id=1, source_target_pairs={{0,1},{1,2},{2,3},{3,4},{4,5},{5,6},{6,7},{7,8},{8,9},{9,10},{10,1... | collective-permute-start | bytes 589832 | tf_op jit(solution)/shard_map/ppermute | solution.py:14
  250.6 26.5 %collective-permute-start.43 = (f32[3,16384]{1,0:T(4,128)}, f32[3,16384]{1,0:T(4,128)}, u32[]{:S(2)}, u32[]{:S(2)}) collective-permute-start(f32[3,16384]{1,0:T(4,128)} %fusion.324), channel_id=1, source_target_pairs={{0,2},{1,3},{2,4},{3,5},{4,6},{5,7},{6,8},{7,9},{8,10},{9,11},{10,... | collective-permute-start | bytes 589832 | tf_op jit(solution)/shard_map/ppermute | solution.py:14
  253.2 37.2 %collective-permute-start.16 = (f32[3,16384]{1,0:T(4,128)}, f32[3,16384]{1,0:T(4,128)}, u32[]{:S(2)}, u32[]{:S(2)}) collective-permute-start(f32[3,16384]{1,0:T(4,128)} %fusion.363), channel_id=1, source_target_pairs={{0,31},{1,0},{2,1},{3,2},{4,3},{5,4},{6,5},{7,6},{8,7},{9,8},{10,9... | collective-permute-start | bytes 589832 | tf_op jit(solution)/shard_map/ppermute | solution.py:14
  260.4 16.7 %copy-start.38 = (f32[3,16384]{1,0:T(4,128)}, f32[3,16384]{1,0:T(4,128)S(1)}, u32[]{:S(2)}) copy-start(f32[3,16384]{1,0:T(4,128)S(1)} %collective-permute-done.40) | copy-start | bytes 589828
  260.4 30.1 %collective-permute-start.17 = (f32[3,16384]{1,0:T(4,128)}, f32[3,16384]{1,0:T(4,128)}, u32[]{:S(2)}, u32[]{:S(2)}) collective-permute-start(f32[3,16384]{1,0:T(4,128)} %fusion.352), channel_id=1, source_target_pairs={{0,30},{1,31},{2,0},{3,1},{4,2},{5,3},{6,4},{7,5},{8,6},{9,7},{10,... | collective-permute-start | bytes 589832 | tf_op jit(solution)/shard_map/ppermute | solution.py:14
  263.0 27.5 %collective-permute-start.18 = (f32[3,16384]{1,0:T(4,128)}, f32[3,16384]{1,0:T(4,128)}, u32[]{:S(2)}, u32[]{:S(2)}) collective-permute-start(f32[3,16384]{1,0:T(4,128)} %fusion.341), channel_id=1, source_target_pairs={{0,1},{1,2},{2,3},{3,4},{4,5},{5,6},{6,7},{7,8},{8,9},{9,10},{10,1... | collective-permute-start | bytes 589832 | tf_op jit(solution)/shard_map/ppermute | solution.py:14
  263.0 27.5 %collective-permute-start.19 = (f32[3,16384]{1,0:T(4,128)}, f32[3,16384]{1,0:T(4,128)}, u32[]{:S(2)}, u32[]{:S(2)}) collective-permute-start(f32[3,16384]{1,0:T(4,128)} %fusion.330), channel_id=1, source_target_pairs={{0,2},{1,3},{2,4},{3,5},{4,6},{5,7},{6,8},{7,9},{8,10},{9,11},{10,... | collective-permute-start | bytes 589832 | tf_op jit(solution)/shard_map/ppermute | solution.py:14
  309.1 9.2 %collective-permute-start.20 = (f32[3,16384]{1,0:T(4,128)}, f32[3,16384]{1,0:T(4,128)S(1)}, u32[]{:S(2)}, u32[]{:S(2)}) collective-permute-start(f32[3,16384]{1,0:T(4,128)} %fusion.362), channel_id=1, source_target_pairs={{0,31},{1,0},{2,1},{3,2},{4,3},{5,4},{6,5},{7,6},{8,7},{9,8},{10,9... | collective-permute-start | bytes 589832 | tf_op jit(solution)/shard_map/ppermute | solution.py:14
  311.8 12.3 %collective-permute-start.21 = (f32[3,16384]{1,0:T(4,128)}, f32[3,16384]{1,0:T(4,128)S(1)}, u32[]{:S(2)}, u32[]{:S(2)}) collective-permute-start(f32[3,16384]{1,0:T(4,128)} %fusion.351), channel_id=1, source_target_pairs={{0,30},{1,31},{2,0},{3,1},{4,2},{5,3},{6,4},{7,5},{8,6},{9,7},{10,... | collective-permute-start | bytes 589832 | tf_op jit(solution)/shard_map/ppermute | solution.py:14
  311.8 12.3 %collective-permute-start.22 = (f32[3,16384]{1,0:T(4,128)}, f32[3,16384]{1,0:T(4,128)S(1)}, u32[]{:S(2)}, u32[]{:S(2)}) collective-permute-start(f32[3,16384]{1,0:T(4,128)} %fusion.340), channel_id=1, source_target_pairs={{0,1},{1,2},{2,3},{3,4},{4,5},{5,6},{6,7},{7,8},{8,9},{9,10},{10,1... | collective-permute-start | bytes 589832 | tf_op jit(solution)/shard_map/ppermute | solution.py:14
  312.0 13.5 %collective-permute-start.23 = (f32[3,16384]{1,0:T(4,128)S(1)}, f32[3,16384]{1,0:T(4,128)}, u32[]{:S(2)}, u32[]{:S(2)}) collective-permute-start(f32[3,16384]{1,0:T(4,128)S(1)} %fusion.329), channel_id=1, source_target_pairs={{0,2},{1,3},{2,4},{3,5},{4,6},{5,7},{6,8},{7,9},{8,10},{9,11},{10,... | collective-permute-start | bytes 589832 | tf_op jit(solution)/shard_map/ppermute | solution.py:14
  (51 other events, 260.3 us)
Sparse Core Ops, SparseCore 0:
  358.0 67.1 all-gather.2
